TPU v7x, 32 devices: a whole 2x2x4 slice. The times are simulated.
32 devices in a mesh: dp: 32 (over z, y, x, core).
Axes of the slice: x: 2, y: 2, z: 4, core: 2. Of those that a mesh axis runs over, the one named last changes fastest.
Arguments:
- grad_proj: bfloat16 [32, 3, 512, 512], P('dp')
- grad_up: bfloat16 [32, 3, 512, 2048], P('dp')
- err_proj: float32 [32, 3, 512, 512], P('dp')
- err_up: float32 [32, 3, 512, 2048], P('dp')
- q_proj: float32 [3, 512, 64], replicated
- q_up: float32 [3, 2048, 64], replicated
- w_proj: float32 [3, 512, 512], replicated
- w_up: float32 [3, 512, 2048], replicated
- mom_proj: float32 [3, 512, 512], replicated
- mom_up: float32 [3, 512, 2048], replicated
Outputs:
- output 1: float32 [3, 512, 512], replicated
- output 2: float32 [3, 512, 2048], replicated
- output 3: float32 [3, 512, 512], replicated
- output 4: float32 [3, 512, 2048], replicated
- output 5: float32 [3, 512, 64], replicated
- output 6: float32 [3, 2048, 64], replicated
- output 7: float32 [32, 3, 512, 512], P('dp')
- output 8: float32 [32, 3, 512, 2048], P('dp')
All inputs are finite; a program needn't handle non-finite values.
Results may differ from a plain program's by a relative error of at most 0.001.
Values sent between devices are 32-bit elements.
A program may use at most 1 GiB of HBM per device.

v0:
```python
import jax
import jax.numpy as jnp
from jax import lax
from jax.sharding import PartitionSpec as P

MOMENTUM = 0.9
LEARN_RATE = 0.1
PRECISE = lax.Precision.HIGHEST


def orthonormalize(p_mat):
    col_ids = jnp.arange(p_mat.shape[1])

    def gs_step(index, p_cur):
        col_vec = lax.dynamic_slice_in_dim(p_cur, index, 1, axis=1)
        unit_vec = col_vec / jnp.sqrt(jnp.sum(col_vec * col_vec))
        coeffs = jnp.sum(unit_vec * p_cur, axis=0, keepdims=True)
        later = (col_ids > index)[None, :]
        p_cur = p_cur - unit_vec * jnp.where(later, coeffs, 0.0)
        return jnp.where((col_ids == index)[None, :], unit_vec, p_cur)

    return lax.fori_loop(0, p_mat.shape[1], gs_step, p_mat)


def one_matrix(grad_l, err_l, q_l, w_l, mom_l, num_dev):
    m_loc = grad_l.astype(jnp.float32) + err_l
    p_part = jnp.dot(m_loc, q_l, precision=PRECISE, preferred_element_type=jnp.float32)
    p_mat = orthonormalize(lax.psum(p_part, 'dp') / num_dev)
    q_part = lax.dot_general(m_loc, p_mat, (((0,), (0,)), ((), ())), precision=PRECISE, preferred_element_type=jnp.float32)
    q_new = lax.psum(q_part, 'dp') / num_dev
    g_hat = lax.dot_general(p_mat, q_new, (((1,), (1,)), ((), ())), precision=PRECISE, preferred_element_type=jnp.float32)
    mom_new = MOMENTUM * mom_l + g_hat
    return w_l - LEARN_RATE * mom_new, mom_new, q_new, m_loc - g_hat


def compress_all(grad_all, err_all, q_factor, weights, moment_in, num_dev):
    results = [one_matrix(grad_all[0, layer], err_all[0, layer], q_factor[layer], weights[layer], moment_in[layer], num_dev) for layer in range(grad_all.shape[1])]
    w_new = jnp.stack([res_layer[0] for res_layer in results])
    mom_new = jnp.stack([res_layer[1] for res_layer in results])
    q_new = jnp.stack([res_layer[2] for res_layer in results])
    err_new = jnp.stack([res_layer[3] for res_layer in results])[None]
    return w_new, mom_new, q_new, err_new


def solution(mesh):
    num_dev = mesh.shape['dp']
    dev_spec = P('dp')
    rep_spec = P()

    def local_step(grad_proj, grad_up, err_proj, err_up, q_proj, q_up, w_proj, w_up, mom_proj, mom_up):
        proj = compress_all(grad_proj, err_proj, q_proj, w_proj, mom_proj, num_dev)
        upper = compress_all(grad_up, err_up, q_up, w_up, mom_up, num_dev)
        return (proj[0], upper[0], proj[1], upper[1], proj[2], upper[2], proj[3], upper[3])

    in_specs = (dev_spec, dev_spec, dev_spec, dev_spec, rep_spec, rep_spec, rep_spec, rep_spec, rep_spec, rep_spec)
    out_specs = (rep_spec, rep_spec, rep_spec, rep_spec, rep_spec, rep_spec, dev_spec, dev_spec)
    return jax.shard_map(local_step, mesh=mesh, in_specs=in_specs, out_specs=out_specs, check_vma=False)
```

profile of v0, /device:TPU:0, one launch (start us, length us, event | category | flops | bytes accessed | tf_op | source)
XLA Modules:
  0.0 1038.4 jit_solution(11281502809706009729)
XLA Ops:
  7.2 8.1 fusion.14
  15.3 7.4 fusion.20
  22.6 7.5 fusion.26
  30.2 1.8 fusion.35
  32.0 1.8 fusion.41
  33.9 2.0 fusion.47
  35.9 135.2 %all-reduce.7.cloned.1.call-done = (f32[512,64]{0,1:T(8,128)}, f32[512,64]{0,1:T(8,128)}, f32[512,64]{0,1:T(8,128)}, f32[512,64]{0,1:T(8,128)}, f32[512,64]{0,1:T(8,128)}, /*index=5*/f32[512,64]{0,1:T(8,128)}) async-done(((f32[512,64]{0,1:T(8,128)}, f32[512,64]{0,1:T(8,128)}, f32[512,64]{0,1:T(8,128)}, f32[512,64]{0,1:T(8,128)}, f32[512,64]{0,1:T(8,128)}, /*index=5*/f32[512,64]{0,1:T(8,128)}), ...) | async-done | bytes 786448 | tf_op jit(solution)/shard_map/psum | solution.py:28
  171.1 1.0 broadcast_multiply_fusion
  172.1 100.6 %while.95 = (s32[]{:T(128)}, f32[512,64]{0,1:T(8,128)S(1)}, s32[]{:T(128)}) while((s32[]{:T(128)}, f32[512,64]{0,1:T(8,128)S(1)}, s32[]{:T(128)}) %tuple.221), condition=%wide.region_34.35_spmd.clone.clone, body=%wide.region_31.34_spmd.clone.clone.sunk | while | flops 165505 | bytes 404685 | solution.py:22
  172.1 0.6 multiply_reduce_fusion.34
  173.7 0.6 multiply_reduce_fusion.34
  175.3 0.6 multiply_reduce_fusion.34
  176.8 0.6 multiply_reduce_fusion.34
  178.4 0.6 multiply_reduce_fusion.34
  180.0 0.6 multiply_reduce_fusion.34
  181.5 0.6 multiply_reduce_fusion.34
  183.1 0.6 multiply_reduce_fusion.34
  184.7 0.6 multiply_reduce_fusion.34
  186.3 0.6 multiply_reduce_fusion.34
  187.8 0.6 multiply_reduce_fusion.34
  272.7 6.6 fusion.12
  279.4 100.6 %while.94 = (s32[]{:T(128)}, f32[512,64]{0,1:T(8,128)S(1)}, s32[]{:T(128)}) while((s32[]{:T(128)}, f32[512,64]{0,1:T(8,128)S(1)}, s32[]{:T(128)}) %tuple.224), condition=%wide.region_28.29_spmd.clone.clone, body=%wide.region_25.28_spmd.clone.clone.sunk | while | flops 165505 | bytes 404685 | solution.py:22
  380.0 6.6 fusion.18
  386.7 100.6 %while.90 = (s32[]{:T(128)}, f32[512,64]{0,1:T(8,128)S(1)}, s32[]{:T(128)}) while((s32[]{:T(128)}, f32[512,64]{0,1:T(8,128)S(1)}, s32[]{:T(128)}) %tuple.218), condition=%wide.region_4.5_spmd.clone.clone, body=%wide.region_1.4_spmd.clone.clone.sunk | while | flops 165505 | bytes 404685 | solution.py:22
  487.3 2.7 fusion.45
  490.0 100.6 %while.91 = (s32[]{:T(128)}, f32[512,64]{0,1:T(8,128)S(1)}, s32[]{:T(128)}) while((s32[]{:T(128)}, f32[512,64]{0,1:T(8,128)S(1)}, s32[]{:T(128)}) %tuple.215), condition=%wide.region_10.11_spmd.clone.clone, body=%wide.region_7.10_spmd.clone.clone.sunk | while | flops 165505 | bytes 404685 | solution.py:22
  590.6 2.7 fusion.39
  593.4 100.7 %while.93 = (s32[]{:T(128)}, f32[512,64]{0,1:T(8,128)S(1)}, s32[]{:T(128)}) while((s32[]{:T(128)}, f32[512,64]{0,1:T(8,128)S(1)}, s32[]{:T(128)}) %tuple.227), condition=%wide.region_22.23_spmd.clone.clone, body=%wide.region_19.22_spmd.clone.clone.sunk | while | flops 165505 | bytes 404685 | solution.py:22
  694.1 6.6 fusion.24
  700.8 100.9 %while.92 = (s32[]{:T(128)}, f32[512,64]{0,1:T(8,128)S(1)}, s32[]{:T(128)}) while((s32[]{:T(128)}, f32[512,64]{0,1:T(8,128)S(1)}, s32[]{:T(128)}) %tuple.212), condition=%wide.region_16.17_spmd.clone.clone, body=%wide.region_13.16_spmd.clone.clone.sunk | while | flops 165505 | bytes 404685 | solution.py:22
  801.7 2.7 fusion.33
  804.4 135.4 %all-reduce.5.cloned.1.call-done = (f32[512,64]{0,1:T(8,128)}, f32[512,64]{0,1:T(8,128)}, f32[512,64]{0,1:T(8,128)}, f32[2048,64]{0,1:T(8,128)}, f32[2048,64]{0,1:T(8,128)}, /*index=5*/f32[2048,64]{0,1:T(8,128)}) async-done(((f32[512,64]{0,1:T(8,128)}, f32[512,64]{0,1:T(8,128)}, f32[512,64]{0,1:T(8,128)}, f32[2048,64]{0,1:T(8,128)}, f32[2048,64]{0,1:T(8,128)}, /*index=5*/f32[2048,64]{0,1:T(8,128)}), ...) | async-done | bytes 1966096 | tf_op jit(solution)/shard_map/psum | solution.py:30
  939.9 4.7 fusion.57
  944.6 5.0 fusion.59
  949.7 1.0 fusion.75
  950.8 1.0 fusion.77
  951.9 0.8 multiply_bitcast_fusion.2
  952.7 0.7 multiply_bitcast_fusion.5
  953.4 29.3 %fusion.29 = (f32[1,512,2048]{2,1,0:T(8,128)}, f32[1,512,2048]{2,1,0:T(8,128)}, f32[1,512,2048]{2,1,0:T(8,128)}, f32[1,512,2048]{2,1,0:T(8,128)}, f32[1,512,2048...) fusion(f32[3,512,2048]{2,1,0:T(8,128)} %param.29, ...), kind=kOutput, calls=%fused_computation.71 | convolution fusion | flops 827457536 | bytes 90832896 | tf_op jit(solution)/shard_map/dot_general | solution.py:31
  982.6 11.6 %maximum_bitcast_fusion = f32[1,3,512,2048]{3,2,1,0:T(8,128)} fusion(f32[1,512,2048]{2,1,0:T(8,128)} %get-tuple-element.570, f32[1,512,2048]{2,1,0:T(8,128)} %get-tuple-element.569, f32[1,512,2048]{2,1,0:T(8,128)} %get-tuple-element.571), kind=kLoop, calls=%fused_computation.44 | loop fusion | flops 6291456 | bytes 25165824 | tf_op jit(solution)/shard_map/broadcast_in_dim | solution.py:41
  994.3 11.6 %pad_maximum_fusion.1 = f32[3,512,2048]{2,1,0:T(8,128)} fusion(f32[1,512,2048]{2,1,0:T(8,128)} %get-tuple-element.567, f32[1,512,2048]{2,1,0:T(8,128)} %get-tuple-element.566, f32[1,512,2048]{2,1,0:T(8,128)} %get-tuple-element.568), kind=kLoop, calls=%fused_computation.43 | loop fusion | flops 6291456 | bytes 25165824 | tf_op jit(solution)/shard_map/stack | solution.py:39
  1005.9 11.6 %pad_maximum_fusion = f32[3,512,2048]{2,1,0:T(8,128)} fusion(f32[1,512,2048]{2,1,0:T(8,128)} %get-tuple-element.561, f32[1,512,2048]{2,1,0:T(8,128)} %get-tuple-element.562, f32[1,512,2048]{2,1,0:T(8,128)} %get-tuple-element.560), kind=kLoop, calls=%fused_computation.42 | loop fusion | flops 6291456 | bytes 25165824 | tf_op jit(solution)/shard_map/stack | solution.py:38
  1017.5 5.6 fusion.50
  1023.1 2.0 maximum_bitcast_fusion.1
  1025.1 2.0 pad_maximum_fusion.3
  1027.1 2.0 pad_maximum_fusion.2
  1029.0 1.2 pad_maximum_fusion.4
  1030.3 0.8 pad_maximum_fusion.5
  (2335 shorter events, 314.7 us)
Async XLA Ops:
  7.2 163.9 %all-reduce.7.cloned.1.call-start = ((), (), s32[]{:S(2)}) async-start(), calls=%async_computation.1 | async-start | bytes 1572864 | tf_op jit(solution)/shard_map/psum | solution.py:28
  7.2 8.1 copy-start
  22.6 7.5 copy-start.1
  22.6 7.5 copy-start.2
  22.6 7.5 copy-start.11
  35.9 904.0 %all-reduce.5.cloned.1.call-start = ((), (), s32[]{:S(2)}) async-start(), calls=%async_computation | async-start | bytes 3932160 | tf_op jit(solution)/shard_map/psum | solution.py:30
  279.4 107.3 %copy-start.14 = (f32[512,64]{0,1:T(8,128)S(1)}, f32[512,64]{0,1:T(8,128)}, u32[]{:S(2)}) copy-start(f32[512,64]{0,1:T(8,128)} %get-tuple-element.555) | copy-start | bytes 393220
  279.4 107.3 %copy-start.15 = (f32[512,64]{0,1:T(8,128)S(1)}, f32[512,64]{0,1:T(8,128)}, u32[]{:S(2)}) copy-start(f32[512,64]{0,1:T(8,128)} %get-tuple-element.556) | copy-start | bytes 393220
  386.6 206.7 %copy-start.12 = (f32[512,64]{0,1:T(8,128)S(1)}, f32[512,64]{0,1:T(8,128)}, u32[]{:S(2)}) copy-start(f32[512,64]{0,1:T(8,128)} %get-tuple-element.554) | copy-start | bytes 393220
  386.6 206.7 %copy-start.13 = (f32[512,64]{0,1:T(8,128)S(1)}, f32[512,64]{0,1:T(8,128)}, u32[]{:S(2)}) copy-start(f32[512,64]{0,1:T(8,128)} %get-tuple-element.559) | copy-start | bytes 393220
  939.9 4.7 copy-start.5
  939.9 4.7 copy-start.4
  944.6 5.2 copy-start.9
  944.6 6.2 copy-start.8
  944.6 7.2 copy-start.3
  944.6 8.1 copy-start.7
  1027.1 2.0 copy-start.6
  1027.1 3.2 copy-start.10
Sparse Core Ops, SparseCore 0:
  36.0 135.0 all-reduce.6
  804.6 135.2 all-reduce.4
where the time goes:
time: 1050 us; the launch traced here: 1040 us
  other arithmetic  367 us (35%)
  loops' own time  283 us (27%)
  waiting for transfers between devices  271 us (26%)
  matrix products  103 us (10%)
  between operations  14.7 us (1%)
    another operation x6, loops' own time, orthonormalize(): return lax.fori_loop(0, p_mat.shape[1], gs_step, p_mat)  283 us
    reduce_sum x384, other arithmetic, gs_step(): unit_vec = col_vec / jnp.sqrt(jnp.sum(col_vec * col_vec))  234 us
    psum x1, waiting for transfers between devices, one_matrix(): q_new = lax.psum(q_part, 'dp') / num_dev  135 us
    psum x1, waiting for transfers between devices, one_matrix(): p_mat = orthonormalize(lax.psum(p_part, 'dp') / num_dev)  135 us
    dot_general x6, matrix products, one_matrix(): lax.dot_general(p_mat, q_new, (((1,), (1,)), ((), ())), precision=PRECISE...  46.6 us
    reduce_sum x384, other arithmetic, gs_step(): coeffs = jnp.sum(unit_vec * p_cur, axis=0, keepdims=True)  42.8 us
    select_n x384, other arithmetic, gs_step(): return jnp.where((col_ids == index)[None, :], unit_vec, p_cur)  34.2 us
    dot_general x6, matrix products, one_matrix(): jnp.dot(m_loc, q_l, precision=PRECISE, preferred_element_type=jnp.float32)  28.6 us
  transfers between devices with their start and end apart: 2, of which 2 were waited for; matrix products, arithmetic and copies ran while one was open for 0% of the time, Pallas kernels for 0%

commit v1 on v0

v1 whole, which is shorter than its diff:
```python
import jax
import jax.numpy as jnp
from jax import lax
from jax.experimental import pallas as pl
from jax.experimental.pallas import tpu as pltpu
from jax.sharding import PartitionSpec as P

MOMENTUM = 0.9
LEARN_RATE = 0.1
F32 = jnp.float32
BF16 = jnp.bfloat16
MESH = pl.DeviceIdType.MESH
LAYERS = 3
RANK = 64
BLK = 512
HALF = 256
PER_LAYER = 5
CHUNKS = LAYERS * PER_LAYER
SLOTS = 4
VMEM_LIMIT = 14 << 20
P_COLS = 1024
Q_COLS = 2560
NT = (((1,), (1,)), ((), ()))
NN = (((1,), (0,)), ((), ()))


def split3(val):
    one = val.astype(BF16)
    rest = val - one.astype(F32)
    two = rest.astype(BF16)
    three = (rest - two.astype(F32)).astype(BF16)
    return one, two, three


def mxu(lhs, rhs, dims):
    return lax.dot_general(lhs, rhs, dims, preferred_element_type=F32)


def stacked_dot(fac, mat, dims):
    f1, f2, f3 = split3(fac)
    m1, m2, m3 = split3(mat)
    stack = jnp.concatenate([f1, f2, f3], axis=0)
    d1 = mxu(stack, m1, dims)
    d2 = mxu(stack[: 2 * RANK], m2, dims)
    d3 = mxu(stack[:RANK], m3, dims)
    low = d1[2 * RANK :] + d2[RANK:] + d3
    mid = d1[RANK : 2 * RANK] + d2[:RANK]
    return d1[:RANK] + (mid + low)


def full_dot(lhs, rhs, dims):
    return lax.dot_general(lhs, rhs, dims, precision=lax.Precision.HIGHEST, preferred_element_type=F32)


class Unit:
    def __init__(self, place, parts, result, sems, num_dev):
        self.x, self.ra, self.rb, self.rc, self.r = parts + (result,)
        self.ssem, self.rsem = sems
        self.num_dev = num_dev
        self.cols = self.x.shape[1]
        self.zc = self.cols // 4
        self.place = place
        self.sends = []

    def copy(self, src, dst, idx, dev):
        return pltpu.make_async_remote_copy(
            src_ref=src, dst_ref=dst, send_sem=self.ssem.at[idx], recv_sem=self.rsem.at[idx],
            device_id=(dev,), device_id_type=MESH)

    def start(self, cps):
        for cp in cps:
            cp.start()
        self.sends += cps

    def zcols(self, z):
        return pl.ds(pl.multiple_of(z * self.zc, 128), self.zc)

    def stage(self, num):
        p = self.place
        if num == 0:
            self.a = self.copy(self.x.at[pl.ds(p.other_half, 32)], self.ra, 0, p.partner)
            self.start([self.a])
        elif num == 1:
            self.a.wait_recv()
            self.ra[...] += self.x[pl.ds(p.half, 32)]
            self.b = [self.copy(self.ra.at[pl.ds(p.mate_sub[k], 8)], self.rb.at[k], 1 + k, p.mates[k]) for k in range(3)]
            self.start(self.b)
        elif num == 2:
            own = self.ra[pl.ds(p.sub, 8)]
            for cp in self.b:
                cp.wait_recv()
            self.x[pl.ds(p.row, 8)] = (own + self.rb[0]) + (self.rb[1] + self.rb[2])
            self.c = [self.copy(self.x.at[pl.ds(p.row, 8), self.zcols(p.zs[k])], self.rc.at[k], 4 + k, p.zmates[k]) for k in range(3)]
            self.start(self.c)
        elif num == 3:
            own = self.x[pl.ds(p.row, 8), self.zcols(p.z)]
            for cp in self.c:
                cp.wait_recv()
            tot = (own + self.rc[0]) + (self.rc[1] + self.rc[2])
            self.r[pl.ds(p.row, 8), self.zcols(p.z)] = tot * (1.0 / self.num_dev)
            ref = self.r.at[pl.ds(p.row, 8), self.zcols(p.z)]
            self.d = [self.copy(ref, ref, 7 + k, p.zmates[k]) for k in range(3)]
            self.start(self.d)
        elif num == 4:
            for cp in self.d:
                cp.wait_recv()
            ref = self.r.at[pl.ds(p.row, 8)]
            self.e = [self.copy(ref, ref, 10 + k, p.mates[k]) for k in range(3)]
            self.start(self.e)
        elif num == 5:
            for cp in self.e:
                cp.wait_recv()
            ref = self.r.at[pl.ds(p.half, 32)]
            self.f = self.copy(ref, ref, 13, p.partner)
            self.start([self.f])
        else:
            self.f.wait_recv()

    def finish(self):
        for cp in self.sends:
            cp.wait_send()


class Place:
    def __init__(self):
        me = lax.axis_index('dp')
        core, x, y, z = me % 2, (me // 2) % 2, (me // 4) % 2, me // 8
        dx, dy = 2 - 4 * x, 4 - 8 * y
        self.z = z
        self.partner = me + 1 - 2 * core
        self.mates = [me + dx, me + dy, me + dx + dy]
        self.zs = [(z + k) % 4 for k in (1, 2, 3)]
        self.zmates = [me + 8 * (zk - z) for zk in self.zs]
        self.half = pl.multiple_of(core * 32, 32)
        self.other_half = pl.multiple_of(32 - core * 32, 32)
        sub = x + 2 * y
        self.sub = pl.multiple_of(sub * 8, 8)
        self.mate_sub = [pl.multiple_of(((1 - x) + 2 * y) * 8, 8), pl.multiple_of((x + 2 * (1 - y)) * 8, 8),
                         pl.multiple_of(((1 - x) + 2 * (1 - y)) * 8, 8)]
        self.row = pl.multiple_of(core * 32 + sub * 8, 8)


def eliminate(aug):
    rows = RANK
    for base in range(0, rows, 8):
        r = [aug[base + i] for i in range(8)]
        d = {}
        for i in range(8):
            for j in range(i, 8):
                d[i, j] = jnp.broadcast_to(r[i][:, base + j : base + j + 1], (8, 128))
        inv = []
        for i in range(8):
            inv.append(1.0 / d[i, i])
            for j in range(i + 1, 8):
                coef = d[i, j] * inv[i]
                r[j] = r[j] - coef * r[i]
                for k in range(j, 8):
                    d[j, k] = d[j, k] - coef * d[i, k]
        scaled = [r[i] * inv[i] for i in range(8)]
        for t in range(base + 8, rows):
            row = aug[t]
            acc = [None, None]
            for i in range(8):
                term = jnp.broadcast_to(scaled[i][:, t : t + 1], (8, 128)) * r[i]
                acc[i % 2] = term if acc[i % 2] is None else acc[i % 2] + term
            aug[t] = row - (acc[0] + acc[1])
        for i in range(8):
            aug[base + i] = r[i] / jnp.sqrt(d[i, i])
        yield


def orthonormalize(p_src, pt_out, aug, s_ref):
    eye = (lax.broadcasted_iota(jnp.int32, (RANK, 128), 0) + RANK == lax.broadcasted_iota(jnp.int32, (RANK, 128), 1)).astype(F32)
    for rep in range(2):
        for m in range(6, 8):
            aug[:, m, :] = jnp.where(lax.broadcasted_iota(jnp.int32, (RANK, 128), 0) == lax.broadcasted_iota(jnp.int32, (RANK, 128), 1), 1.0, eye)
        for m in range(6):
            pt = p_src(m) if rep == 0 else pt_out[m]
            gram = full_dot(pt, pt, NT)
            aug[:, m, :] = jnp.concatenate([gram, jnp.zeros((RANK, RANK), F32)], axis=1) + eye
        yield
        yield from eliminate(aug)
        for m in range(6):
            s_new = aug[:, m, :][:, RANK:]
            pt = p_src(m) if rep == 0 else pt_out[m]
            pt_out[m] = full_dot(s_new, pt, NN)
            s_ref[m] = s_new if rep == 0 else full_dot(s_new, s_ref[m], NN)
        yield


def reduce_kernel(num_dev, gp, gu, ep, eu, qp, qu, wp, wu, vp, vu,
                  m_out, w_out, v_out, qt_out, pt_out,
                  gbuf, xp, rap, rbp, rcp, rp, xq, raq, rbq, rcq, rq, aug, s_ref,
                  esem, gsem, qsem, wsem, ssem, rsem):
    place = Place()
    barrier = pltpu.get_barrier_semaphore()
    peers = [place.partner] + place.mates + place.zmates
    for dev in peers:
        pl.semaphore_signal(barrier, inc=1, device_id=(dev,), device_id_type=MESH)

    def load(ci):
        l, c, slot = ci // PER_LAYER, ci % PER_LAYER, ci % SLOTS

        @pl.when(c == 0)
        def _():
            pltpu.make_async_copy(ep.at[l], m_out.at[ci], esem.at[slot]).start()
            pltpu.make_async_copy(gp.at[l], gbuf.at[slot], gsem.at[slot]).start()

        @pl.when(c > 0)
        def _():
            cols = pl.ds(pl.multiple_of((c - 1) * BLK, BLK), BLK)
            pltpu.make_async_copy(eu.at[l, :, cols], m_out.at[ci], esem.at[slot]).start()
            pltpu.make_async_copy(gu.at[l, :, cols], gbuf.at[slot], gsem.at[slot]).start()

    qcopies = []
    for l in range(LAYERS):
        for c in range(PER_LAYER):
            ci = l * PER_LAYER + c
            src = qp.at[l] if c == 0 else qu.at[l, :, pl.ds((c - 1) * BLK, BLK)]
            qcopies.append(pltpu.make_async_copy(src, rq.at[l, :, pl.ds(c * BLK, BLK)], qsem.at[ci]))
    for cp in qcopies[:PER_LAYER]:
        cp.start()
    for ci in range(SLOTS):
        load(ci)
    for cp in qcopies[PER_LAYER:]:
        cp.start()

    punit = [Unit(place, (xp.at[l], rap.at[l], rbp.at[l], rcp.at[l]), rp.at[l], (ssem.at[l], rsem.at[l]), num_dev) for l in range(LAYERS)]
    qunit = [Unit(place, (xq.at[l], raq.at[l], rbq.at[l], rcq.at[l]), rq.at[l], (ssem.at[3 + l], rsem.at[3 + l]), num_dev) for l in range(LAYERS)]

    def p_layer(l):
        xp[l] = jnp.zeros((RANK, P_COLS), F32)
        for c in range(PER_LAYER):
            qcopies[l * PER_LAYER + c].wait()

        @pl.loop(0, PER_LAYER)
        def _(c):
            ci = l * PER_LAYER + c
            slot = ci % SLOTS
            pltpu.make_async_copy(ep.at[0], m_out.at[ci], esem.at[slot]).wait()
            pltpu.make_async_copy(gp.at[0], gbuf.at[slot], gsem.at[slot]).wait()
            mat = m_out[ci] + gbuf[slot].astype(F32)
            m_out[ci] = mat
            cols = pl.ds(pl.multiple_of(jnp.minimum(c, 1) * BLK, BLK), BLK)
            fac = rq[l, :, pl.ds(pl.multiple_of(c * BLK, BLK), BLK)]
            xp[l, :, cols] += stacked_dot(fac, mat, NT)

            @pl.when(ci + SLOTS < CHUNKS)
            def _():
                load(ci + SLOTS)

    def q_layer(l):
        @pl.loop(0, PER_LAYER)
        def _(c):
            ci = l * PER_LAYER + c
            cols = pl.ds(pl.multiple_of(jnp.minimum(c, 1) * BLK, BLK), BLK)
            out = pl.ds(pl.multiple_of(c * BLK, BLK), BLK)
            xq[l, :, out] = stacked_dot(rp[l, :, cols], m_out[ci], NN)

    wcopies = []
    for l in range(LAYERS):
        for c in range(PER_LAYER):
            ci = l * PER_LAYER + c
            for t, (sp, su, dst) in enumerate(((wp, wu, w_out), (vp, vu, v_out))):
                src = sp.at[l] if c == 0 else su.at[l, :, pl.ds((c - 1) * BLK, BLK)]
                wcopies.append(pltpu.make_async_copy(src, dst.at[ci], wsem.at[2 * ci + t]))

    p_layer(0)
    pl.semaphore_wait(barrier, len(peers))
    punit[0].stage(0)
    p_layer(1)
    punit[0].stage(1)
    punit[1].stage(0)
    p_layer(2)
    punit[0].stage(2)
    punit[1].stage(1)
    punit[2].stage(0)
    for cp in wcopies:
        cp.start()
    for tick in range(4):
        punit[0].stage(tick + 3)
        punit[1].stage(tick + 2)
        punit[2].stage(tick + 1)
    q_layer(0)
    qunit[0].stage(0)
    punit[1].stage(6)
    punit[2].stage(5)
    q_layer(1)
    qunit[1].stage(0)
    qunit[0].stage(1)
    punit[2].stage(6)
    q_layer(2)
    qunit[2].stage(0)
    qunit[1].stage(1)
    qunit[0].stage(2)

    def p_src(m):
        return rp[m // 2, :, (m % 2) * BLK : (m % 2) * BLK + BLK]

    work = orthonormalize(p_src, pt_out, aug, s_ref)
    steps = []
    for tick in range(6):
        for l in range(LAYERS):
            num = tick + 3 - l
            if num <= 6:
                steps.append((l, num))
    for l, num in steps:
        next(work, None)
        qunit[l].stage(num)
    for _ in work:
        pass
    for l in range(LAYERS):
        for c in range(PER_LAYER):
            qt_out[l * PER_LAYER + c] = full_dot(s_ref[2 * l + min(c, 1)], rq[l, :, c * BLK : (c + 1) * BLK], NN)
    for unit in punit + qunit:
        unit.finish()
    for cp in wcopies:
        cp.wait()


def apply_kernel(m_in, w_in, v_in, qt_in, pt_in, wp, wu, vp, vu, qp, qu, ep, eu, lhs, buf, sem, qsem):
    qcopies = []
    for l in range(LAYERS):
        for c in range(PER_LAYER):
            ci = l * PER_LAYER + c
            dst = qp.at[l] if c == 0 else qu.at[l, :, pl.ds((c - 1) * BLK, BLK)]
            qcopies.append(pltpu.make_async_copy(qt_in.at[ci], dst, qsem.at[ci]))
    for cp in qcopies:
        cp.start()

    @pl.loop(0, 2 * LAYERS)
    def _(m):
        p1, p2, p3 = [t.astype(F32) for t in split3(pt_in[m])]
        for t, (a, b) in enumerate(((p1, p1), (p2, p1), (p2, p3))):
            lhs[m, :, 128 * t : 128 * t + 128] = jnp.transpose(jnp.concatenate([a, b], axis=0)).astype(BF16)

    outs = ((ep, eu), (vp, vu), (wp, wu))

    @pl.loop(0, 2 * CHUNKS)
    def _(step):
        ci, slot = step // 2, step % SLOTS
        l, c = ci // PER_LAYER, ci % PER_LAYER
        rows = pl.ds(pl.multiple_of((step % 2) * HALF, HALF), HALF)

        @pl.when(step >= SLOTS)
        def _():
            for t in range(3):
                pltpu.make_async_copy(buf.at[slot, t], ep.at[0, pl.ds(0, HALF)], sem.at[slot, t]).wait()

        q1, q2, q3 = split3(qt_in[ci])
        rhs = jnp.concatenate([q1, q2, q1, q3, q2, q1], axis=0)
        hat = mxu(lhs[2 * l + jnp.minimum(c, 1), rows], rhs, NN)
        buf[slot, 0] = m_in[ci, rows] - hat
        mom = MOMENTUM * v_in[ci, rows] + hat
        buf[slot, 1] = mom
        buf[slot, 2] = w_in[ci, rows] - LEARN_RATE * mom

        @pl.when(c == 0)
        def _():
            for t in range(3):
                pltpu.make_async_copy(buf.at[slot, t], outs[t][0].at[l, rows], sem.at[slot, t]).start()

        @pl.when(c > 0)
        def _():
            cols = pl.ds(pl.multiple_of((c - 1) * BLK, BLK), BLK)
            for t in range(3):
                pltpu.make_async_copy(buf.at[slot, t], outs[t][1].at[l, rows, cols], sem.at[slot, t]).start()

    for slot in range(SLOTS):
        for t in range(3):
            pltpu.make_async_copy(buf.at[slot, t], ep.at[0, pl.ds(0, HALF)], sem.at[slot, t]).wait()
    for cp in qcopies:
        cp.wait()


def solution(mesh):
    num_dev = mesh.shape['dp']
    dev_spec, rep_spec = P('dp'), P()
    sds = jax.ShapeDtypeStruct
    hbm, vmem = pl.BlockSpec(memory_space=pltpu.HBM), pl.BlockSpec(memory_space=pltpu.VMEM)
    big = pltpu.VMEM((CHUNKS, BLK, BLK), F32)

    def bufs(cols):
        return [pltpu.VMEM((LAYERS, RANK, cols), F32), pltpu.VMEM((LAYERS, 32, cols), F32),
                pltpu.VMEM((LAYERS, 3, 8, cols), F32), pltpu.VMEM((LAYERS, 3, 8, cols // 4), F32),
                pltpu.VMEM((LAYERS, RANK, cols), F32)]

    def local_step(grad_p, grad_u, err_p, err_u, q_p, q_u, w_p, w_u, mom_p, mom_u):
        m_all, w_all, v_all, qt, pt = pl.pallas_call(
            lambda *refs: reduce_kernel(num_dev, *refs),
            out_shape=[big, big, big, pltpu.VMEM((CHUNKS, RANK, BLK), F32), pltpu.VMEM((2 * LAYERS, RANK, BLK), F32)],
            in_specs=[hbm] * 10,
            out_specs=[vmem] * 5,
            scratch_shapes=[pltpu.VMEM((SLOTS, BLK, BLK), BF16)]
            + bufs(P_COLS) + bufs(Q_COLS)
            + [pltpu.VMEM((RANK, 8, 128), F32), pltpu.VMEM((2 * LAYERS, RANK, RANK), F32),
               pltpu.SemaphoreType.DMA((SLOTS,)), pltpu.SemaphoreType.DMA((SLOTS,)),
               pltpu.SemaphoreType.DMA((CHUNKS,)), pltpu.SemaphoreType.DMA((2 * CHUNKS,)),
               pltpu.SemaphoreType.DMA((6, 14)), pltpu.SemaphoreType.DMA((6, 14))],
            compiler_params=pltpu.CompilerParams(collective_id=0, has_side_effects=True, vmem_limit_bytes=VMEM_LIMIT),
            name='reduce_factors',
        )(grad_p[0], grad_u[0], err_p[0], err_u[0], jnp.swapaxes(q_p, 1, 2), jnp.swapaxes(q_u, 1, 2), w_p, w_u, mom_p, mom_u)
        small, wide = sds((LAYERS, BLK, BLK), F32), sds((LAYERS, BLK, 4 * BLK), F32)
        w_pn, w_un, v_pn, v_un, q_pn, q_un, e_pn, e_un = pl.pallas_call(
            apply_kernel,
            out_shape=[small, wide, small, wide, sds((LAYERS, RANK, BLK), F32), sds((LAYERS, RANK, 4 * BLK), F32), small, wide],
            in_specs=[vmem] * 5,
            out_specs=[hbm] * 8,
            scratch_shapes=[pltpu.VMEM((2 * LAYERS, BLK, 384), BF16), pltpu.VMEM((SLOTS, 3, HALF, BLK), F32),
                            pltpu.SemaphoreType.DMA((SLOTS, 3)), pltpu.SemaphoreType.DMA((CHUNKS,))],
            compiler_params=pltpu.CompilerParams(vmem_limit_bytes=VMEM_LIMIT),
            name='apply_factors',
        )(*[pltpu.with_memory_space_constraint(t, pltpu.VMEM) for t in (m_all, w_all, v_all, qt, pt)])
        return (w_pn, w_un, v_pn, v_un, jnp.swapaxes(q_pn, 1, 2), jnp.swapaxes(q_un, 1, 2), e_pn[None], e_un[None])

    in_specs = (dev_spec,) * 4 + (rep_spec,) * 6
    out_specs = (rep_spec,) * 6 + (dev_spec,) * 2
    return jax.shard_map(local_step, mesh=mesh, in_specs=in_specs, out_specs=out_specs, check_vma=False)
```

time: 1050 us -> 92.2 us (0.09); the launches traced: 1040 us -> 91.4 us
  other arithmetic: 367 us -> 0 us
  loops' own time: 283 us -> 0 us
  waiting for transfers between devices: 271 us -> 0 us
  matrix products: 103 us -> 0 us
  Pallas kernels: 0 us -> 90.6 us
  between operations: 14.7 us -> 0.81 us
    another operation x6 -> x0, loops' own time: 283 us -> none  [orthonormalize(): return lax.fori_loop(0, p_mat.shape[1], gs_step, p_mat)]
    reduce_sum x768 -> x0, other arithmetic: 277 us -> none  [the longest x384 234 us: gs_step(): unit_vec = col_vec / jnp.sqrt(jnp.sum(col_vec * col_vec))]
    psum x2 -> x0, waiting for transfers between devices: 271 us -> none  [the longest x1 135 us: one_matrix(): q_new = lax.psum(q_part, 'dp') / num_dev]
    dot_general x18 -> x0, matrix products: 103 us -> none  [the longest x6 46.6 us: one_matrix(): lax.dot_general(p_mat, q_new, (((1,), (1,)), ((), ())), precision=PRECISE...]
    pallas_call x0 -> x2, Pallas kernels: none -> 90.6 us  [the longest x1 74 us: local_step(): pl.pallas_call(lambda *refs: reduce_kernel(num_dev, *refs), out_shape=[bi...]
    select_n x768 -> x0, other arithmetic: 36.6 us -> none  [the longest x384 34.2 us: gs_step(): return jnp.where((col_ids == index)[None, :], unit_vec, p_cur)]
    another operation x12 -> x0, other arithmetic: 30.8 us -> none  [the longest x2 13.6 us: compress_all(): w_new = jnp.stack([res_layer[0] for res_layer in results])]
    broadcast_in_dim x2 -> x0, other arithmetic: 13.6 us -> none  [compress_all(): err_new = jnp.stack([res_layer[3] for res_layer in results])[None]]
  transfers between devices with their start and end apart: 2 -> 0, of which waited for: 2 -> 0; matrix products, arithmetic and copies ran while one was open for 0% -> 0% of each run, Pallas kernels for 0% -> 0%
where the time goes in v1:
time: 92.2 us; the launch traced here: 91.4 us
  Pallas kernels  90.6 us (98%)
    pallas_call x1, Pallas kernels, local_step(): pl.pallas_call(lambda *refs: reduce_kernel(num_dev, *refs), out_shape=[bi...  74 us
    pallas_call x1, Pallas kernels, local_step(): pl.pallas_call(apply_kernel, out_shape=[small, wide, small, wide, sds((LA...  16.6 us

profile of v1, /device:TPU:0, one launch (start us, length us, event | category | flops | bytes accessed | tf_op | source)
XLA Modules:
  0.0 91.4 jit_solution(16428375190992238793)
XLA Ops:
  0.6 74.0 %reduce_factors.1 = (f32[15,512,512]{2,1,0:T(8,128)S(1)}, f32[15,512,512]{2,1,0:T(8,128)S(1)}, f32[15,512,512]{2,1,0:T(8,128)S(1)}, f32[15,64,512]{2,1,0:T(8,128)S(1)}, f32[6,64,512]{2,1,0:T(8,128)S(1)}) custom-call(bf16[3,512,512]{2,1,0:T(8,128)(2,1)} %bitcast.13, bf16[3,512,2048]{2,1,0:T(8,128)(2,1)} %bitcast.11, f32[3,512,512]{2,1,0:T(8,128)} %bitcast.12, ...), custom_call_target="tpu_custom_call" | custom-call | tf_op jit(solution)/shard_map/reduce_factors/pallas_call | solution.py:389
  74.6 16.6 %apply_factors.1 = (f32[3,512,512]{2,1,0:T(8,128)}, f32[3,512,2048]{2,1,0:T(8,128)}, f32[3,512,512]{2,1,0:T(8,128)}, f32[3,512,2048]{2,1,0:T(8,128)}, f32[3,64,5...) custom-call(f32[15,512,512]{2,1,0:T(8,128)S(1)} %get-tuple-element.21.m_in, ...), custom_call_target="tpu_custom_call" | custom-call | tf_op jit(solution)/shard_map/apply_factors/pallas_call | solution.py:404
